TPU v7x, 32 devices: a whole 2x2x4 slice. The times are simulated.
32 devices in a mesh: seq: 8 (over y, x, core), head: 4 (over z).
Axes of the slice: x: 2, y: 2, z: 4, core: 2. Of those that a mesh axis runs over, the one named last changes fastest.
Arguments:
- span_order: int32 [16], replicated, may hold values from 0 to 15, each once
- queries: bfloat16 [1024, 36864], P('seq', 'head'), may hold values from -32 to 32
- latent_kv: bfloat16 [1024, 576], P(('seq', 'head')), may hold values from -8 to 8
- w_uv: bfloat16 [64, 512, 128], P('head'), may hold values from -0.25 to 0.25
Outputs:
- attended: bfloat16 [1024, 8192], P('seq', 'head')
Inputs may be any that keep to these rules, and one draw needn't show every extreme that they name: `span_order`: each of 0 to 15 appears once.
All inputs are finite; a program needn't handle non-finite values.
Results may differ from a plain program's by a relative error of at most 0.0065.
Values may be sent and summed in bfloat16 or wider, within the bound.
A program may use at most 128 MiB of HBM per device.

v0:
```python
import functools
import math

import jax
import jax.numpy as jnp
import numpy as np
from jax import lax
from jax.experimental import pallas as pl
from jax.experimental.pallas import tpu as pltpu
from jax.sharding import PartitionSpec as P

ROPE_DIM = 64
NOPE_DIM = 128
SEQS = 2
LANES = 128
CHUNK_SPANS = 8
GATHER_MIB = 24
ATTEND_MIB = 40

theta_base = 10000.0
logit_scale = (NOPE_DIM + ROPE_DIM) ** -0.5


def angle_table(count, half):
    freq = np.exp(-math.log(theta_base) * np.arange(half, dtype=np.float32) / half).astype(
        np.float32
    )
    phases = (np.arange(count, dtype=np.float32)[:, None] * freq[None, :]).astype(np.float64)
    cosine, sine = np.cos(phases), np.sin(phases)
    return np.concatenate([cosine, cosine, -sine, sine], 1).astype(np.float32)


def flip(index, bits):
    out = index
    place = 1
    while place <= bits:
        if bits & place:
            out = out + place * (1 - 2 * ((index // place) % 2))
        place *= 2
    return out


def rotate_tile(tile, table, high):
    lane = lax.broadcasted_iota(jnp.int32, tile.shape, tile.ndim - 1)
    quarter = lane // (ROPE_DIM // 2)
    last = tile.ndim - 1
    forward = pltpu.roll(tile, ROPE_DIM // 2, last)
    backward = pltpu.roll(tile, LANES - ROPE_DIM // 2, last)
    swapped = jnp.where(quarter % 2 == 0, backward, forward)
    turned = pltpu.roll(table, ROPE_DIM, 1)
    cosine, sine = (turned, table) if high else (table, turned)
    here = (quarter >= 2) if high else (quarter < 2)
    return jnp.where(here, tile * cosine + swapped * sine, tile)


def span_places(order_ref, s, spans_seq, span_len):
    seq_first, place = [], []
    for span in range(2):
        mine = order_ref[2 * s + span]
        first = jnp.int32(0)
        for later in range(1, SEQS):
            first = jnp.where(mine >= later * spans_seq, later * spans_seq, first)
        seq_first.append(first)
        place.append((mine - first) * span_len)
    return seq_first, place


def gather_kernel(
    dims,
    latent_ref,
    kv,
    z_send,
    z_recv,
    p_send,
    p_recv,
    d_send,
    d_recv,
):
    n_seq, n_head, heads, rank, span_len, kv_count, spans_seq = dims
    s = lax.axis_index("seq")
    h = lax.axis_index("head")

    def device(seq, head):
        return {"seq": seq, "head": head}

    hops = [1 << b for b in range(1, (n_seq - 1).bit_length())]
    far = range(2, n_seq, 2)

    def last_hop(k, d):
        bits = [b for b in hops if d & b]
        return d

    mesh_id = pl.DeviceIdType.MESH
    barrier = pltpu.get_barrier_semaphore()
    peers = [(s, flip(h, k)) for k in range(1, n_head)]
    peers += [(flip(s, d), h) for d in far]
    peers += [(flip(s, 1), h)]
    for seq, head in peers:
        pl.semaphore_signal(barrier, inc=1, device_id=device(seq, head), device_id_type=mesh_id)
    kv[s * n_head + h] = latent_ref[...]
    pl.semaphore_wait(barrier, len(peers))

    sent = []

    def go(d, k, send, recv, seq, head):
        block = kv.at[flip(s, d) * n_head + flip(h, k)]
        copy = pltpu.make_async_remote_copy(
            src_ref=block if d or k else latent_ref,
            dst_ref=block,
            send_sem=send,
            recv_sem=recv,
            device_id=device(seq, head),
            device_id_type=mesh_id,
        )
        copy.start()
        sent.append(copy)

    def arrived(d, k, send, recv):
        block = kv.at[flip(s, d) * n_head + flip(h, k)]
        pltpu.make_async_remote_copy(
            src_ref=block,
            dst_ref=block,
            send_sem=send,
            recv_sem=recv,
            device_id=device(flip(s, 1), h),
            device_id_type=mesh_id,
        ).wait_recv()

    def spread(k, d):
        for to in reversed(far):
            hop = last_hop(k, to)
            if to - hop == d:
                go(d, k, p_send.at[k, to // 2], p_recv.at[k, to // 2], flip(s, hop), h)
        go(d, k, d_send.at[k, d // 2], d_recv.at[k, d // 2], flip(s, 1), h)

    for k in range(1, n_head):
        go(0, 0, z_send.at[k - 1], z_recv.at[k - 1], s, flip(h, k))
    events = [((k + bin(d).count("1") + 2) if d else k, d, k) for k in range(n_head) for d in range(0, n_seq, 2)]
    for _, d, k in sorted(events):
        if d:
            arrived(d, k, p_send.at[k, d // 2], p_recv.at[k, d // 2])
        elif k:
            arrived(0, k, z_send.at[k - 1], z_recv.at[k - 1])
        spread(k, d)
    for _, d, k in sorted(events):
        arrived(d + 1, k, d_send.at[k, d // 2], d_recv.at[k, d // 2])
    for copy in sent:
        copy.wait_send()


def attend_kernel(
    dims, order_ref, queries_ref, kv, table, w_ref, out_ref, q_rows, keys, mixed, state
):
    n_seq, n_head, heads, rank, span_len, kv_count, spans_seq = dims
    width = rank + ROPE_DIM
    pairs = heads // 2
    s = lax.axis_index("seq")
    spans = SEQS * spans_seq
    per_span = span_len // kv_count
    seq_first, place = span_places(order_ref, s, spans_seq, span_len)
    for span in range(2):
        angles = table[pl.ds(place[span], span_len), :]
        for par in range(2):
            for pair in range(pairs):
                source = pl.ds(span * span_len, span_len)
                first = pair * 2 * width + par * rank
                rows = pl.ds(pair * span_len, span_len)
                tiles = [
                    queries_ref[source, pl.ds(first + c, LANES)] for c in range(0, rank + 1, LANES)
                ]
                tiles[-1] = rotate_tile(
                    tiles[-1].astype(jnp.float32), angles, bool(par)
                ).astype(jnp.bfloat16)
                q_rows[span, par, rows, :] = jnp.concatenate(tiles, 1)

    def block_of(stream_span):
        def pick(slot, found):
            return jnp.where(order_ref[slot] == stream_span, slot * per_span, found)

        if spans > 16:
            return lax.fori_loop(0, spans, pick, jnp.int32(0))
        found = jnp.int32(0)
        for slot in range(spans):
            found = pick(slot, found)
        return found

    chunk_spans = min(CHUNK_SPANS, spans_seq)
    n_chunks = spans_seq // chunk_spans
    chunk = chunk_spans * span_len

    for span in range(2):
        def one_chunk(c, span=span):
            for j in range(chunk_spans):
                block = block_of(seq_first[span] + c * chunk_spans + j)
                raw = kv[pl.ds(block, per_span)].reshape(span_len, width)
                angles = table[pl.ds((c * chunk_spans + j) * span_len, span_len), :]
                pad = jnp.zeros((span_len, LANES - ROPE_DIM), jnp.float32)
                rope = jnp.concatenate([raw[:, rank:].astype(jnp.float32), pad], 1)
                rope = rotate_tile(rope, angles, False)
                rows = pl.ds(j * span_len, span_len)
                keys[0, rows, :rank] = raw[:, :rank]
                keys[0, rows, rank:] = rope.astype(jnp.bfloat16)
                whole = jnp.concatenate([raw[:, :rank].astype(jnp.float32), rope], 1)
                keys[1, rows, :] = pltpu.roll(whole, ROPE_DIM, 1).astype(jnp.bfloat16)
            limit = lax.broadcasted_iota(jnp.int32, (span_len, chunk), 0) + place[span]
            seen = lax.broadcasted_iota(jnp.int32, (span_len, chunk), 1) + c * chunk <= limit
            for par in range(2):
                scores = (
                    lax.dot_general(
                        q_rows[span, par],
                        keys[par],
                        (((1,), (1,)), ((), ())),
                        preferred_element_type=jnp.float32,
                    )
                    * logit_scale
                )
                scores = jnp.where(
                    seen[None], scores.reshape(pairs, span_len, chunk), -jnp.inf
                ).reshape(pairs * span_len, chunk)
                top = jnp.max(scores, 1, keepdims=True)
                if n_chunks > 1:
                    old_top = state[par, :, 0:1]
                    top = jnp.maximum(top, old_top)
                    shrink = jnp.exp(old_top - top)
                expo = jnp.exp(scores - top)
                total = jnp.sum(expo, 1, keepdims=True)
                sums = jnp.dot(
                    expo.astype(jnp.bfloat16),
                    keys[0, :, :rank],
                    preferred_element_type=jnp.float32,
                )
                if n_chunks > 1:
                    total = state[par, :, LANES : LANES + 1] * shrink + total
                    sums = state[par, :, 2 * LANES :] * shrink + sums
                    state[par, :, :LANES] = jnp.broadcast_to(top, (pairs * span_len, LANES))
                    state[par, :, LANES : 2 * LANES] = jnp.broadcast_to(
                        total, (pairs * span_len, LANES)
                    )
                    state[par, :, 2 * LANES :] = sums
                else:
                    finish(par, sums, total)

        def finish(par, sums, total, span=span):
            result = (sums / total).astype(jnp.bfloat16)
            mixed[par, :, pl.ds(span * span_len, span_len), :] = result.reshape(
                pairs, span_len, rank
            )

        if n_chunks == 1:
            one_chunk(0)
        else:
            state[:, :, :LANES] = jnp.full((2, pairs * span_len, LANES), -1e30, jnp.float32)
            state[:, :, LANES:] = jnp.zeros((2, pairs * span_len, LANES + rank), jnp.float32)

            @pl.loop(0, n_chunks)
            def _(c):
                one_chunk(c)

            for par in range(2):
                finish(par, state[par, :, 2 * LANES :], state[par, :, LANES : LANES + 1])

    v_dim = w_ref.shape[2]
    for head in range(heads):
        out_ref[:, pl.ds(head * v_dim, v_dim)] = jnp.dot(
            mixed[head % 2, head // 2], w_ref[head], preferred_element_type=jnp.float32
        ).astype(jnp.bfloat16)


def per_device(n_seq, n_head, span_order, queries, latent_kv, w_uv):
    tok_dev = queries.shape[0]
    heads, rank, v_dim = w_uv.shape
    kv_count, width = latent_kv.shape
    span_len = tok_dev // 2
    spans = span_order.shape[0]
    spans_seq = spans // SEQS
    seq_len = spans_seq * span_len
    pairs = heads // 2
    wide = rank + LANES
    chunk_spans = min(CHUNK_SPANS, spans_seq)
    state_rows = pairs * span_len if spans_seq > chunk_spans else 8
    dims = (n_seq, n_head, heads, rank, span_len, kv_count, spans_seq)
    table = jnp.asarray(angle_table(seq_len, ROPE_DIM // 2))
    dma = pltpu.SemaphoreType.DMA
    smem = pl.BlockSpec(memory_space=pltpu.SMEM)
    vmem = pl.BlockSpec(memory_space=pltpu.VMEM)
    kv = pl.pallas_call(
        functools.partial(gather_kernel, dims),
        out_shape=jax.ShapeDtypeStruct((n_seq * n_head, kv_count, width), jnp.bfloat16),
        in_specs=[vmem],
        out_specs=vmem,
        scratch_shapes=[
            dma((max(n_head - 1, 1),)),
            dma((max(n_head - 1, 1),)),
            dma((n_head, n_seq // 2)),
            dma((n_head, n_seq // 2)),
            dma((n_head, n_seq // 2)),
            dma((n_head, n_seq // 2)),
        ],
        compiler_params=pltpu.CompilerParams(
            collective_id=0, has_side_effects=True, vmem_limit_bytes=GATHER_MIB << 20
        ),
        cost_estimate=pl.CostEstimate(flops=20 << 30, bytes_accessed=1 << 20, transcendentals=0),
        name="gather_keys",
    )(latent_kv)
    return pl.pallas_call(
        functools.partial(attend_kernel, dims),
        out_shape=jax.ShapeDtypeStruct((tok_dev, heads * v_dim), jnp.bfloat16),
        in_specs=[smem, vmem, vmem, vmem, vmem],
        out_specs=vmem,
        scratch_shapes=[
            pltpu.VMEM((2, 2, pairs * span_len, wide), jnp.bfloat16),
            pltpu.VMEM((2, chunk_spans * span_len, wide), jnp.bfloat16),
            pltpu.VMEM((2, pairs, tok_dev, rank), jnp.bfloat16),
            pltpu.VMEM((2, state_rows, 2 * LANES + rank), jnp.float32),
        ],
        compiler_params=pltpu.CompilerParams(vmem_limit_bytes=ATTEND_MIB << 20),
        cost_estimate=pl.CostEstimate(flops=4 << 30, bytes_accessed=8 << 20, transcendentals=1 << 20),
        name="attend",
    )(span_order, queries, kv, table, w_uv)


def solution(mesh):
    in_specs = (P(), P("seq", "head"), P(("seq", "head"), None), P("head", None, None))
    return jax.shard_map(
        functools.partial(per_device, mesh.shape["seq"], mesh.shape["head"]),
        mesh=mesh,
        in_specs=in_specs,
        out_specs=P("seq", "head"),
        check_vma=False,
    )
```

profile of v0, /device:TPU:0, one launch (start us, length us, event | category | flops | bytes accessed | tf_op | source)
XLA Modules:
  0.0 23.2 jit_solution(5343401069681802696)
XLA Ops:
  0.0 0.0 copy-start.1
  0.0 0.0 copy-start
  0.0 0.0 copy-start.2
  0.0 0.9 %copy-done.2 = bf16[32,576]{1,0:T(8,128)(2,1)S(1)} copy-done((bf16[32,576]{1,0:T(8,128)(2,1)S(1)}, bf16[32,576]{1,0:T(8,128)(2,1)}, u32[]{:S(2)}) %copy-start.2) | copy-done | bytes 36888
  0.9 0.0 copy-start.3
  0.9 0.0 copy-start.4
  0.9 16.4 %gather_keys.1.kv = bf16[32,32,576]{2,1,0:T(8,128)(2,1)S(1)} custom-call(bf16[32,576]{1,0:T(8,128)(2,1)S(1)} %copy-done.2), custom_call_target="tpu_custom_call" | custom-call | flops 21474836480 | bytes 1048576 | tf_op jit(solution)/shard_map/gather_keys/pallas_call | solution.py:286
  17.3 0.0 copy-done.1
  17.3 0.0 copy-done
  17.3 0.0 copy-done.3
  17.3 0.0 copy-done.4
  17.3 5.9 %attend.1 = bf16[128,2048]{1,0:T(8,128)(2,1)} custom-call(s32[16]{0:T(128)S(1)} %copy-done.3, bf16[128,9216]{1,0:T(8,128)(2,1)S(1)} %copy-done, bf16[32,32,576]{2,1,0:T(8,128)(2,1)S(1)} %gather_keys.1.kv, f32[512,128]{1,0:T(8,128)S(1)} %copy-done.4, bf16[16,512,128]{2,1,0:T(8,128)(2,1)S(1)} %copy-done.1), custom_call_target="tpu_custom_call" | custom-call | flops 4294967296 | bytes 8388608 | tf_op jit(solution)/shard_map/attend/pallas_call | solution.py:305
Async XLA Ops:
  0.0 17.3 %copy-start.1 = (bf16[16,512,128]{2,1,0:T(8,128)(2,1)S(1)}, bf16[16,512,128]{2,1,0:T(8,128)(2,1)}, u32[]{:S(2)}) copy-start(bf16[16,512,128]{2,1,0:T(8,128)(2,1)} %w_ref.1) | copy-start | bytes 6291460
  0.0 17.3 %copy-start = (bf16[128,9216]{1,0:T(8,128)(2,1)S(1)}, bf16[128,9216]{1,0:T(8,128)(2,1)}, u32[]{:S(2)}) copy-start(bf16[128,9216]{1,0:T(8,128)(2,1)} %queries_ref.1) | copy-start | bytes 7077892
  0.0 0.9 %copy-start.2 = (bf16[32,576]{1,0:T(8,128)(2,1)S(1)}, bf16[32,576]{1,0:T(8,128)(2,1)}, u32[]{:S(2)}) copy-start(bf16[32,576]{1,0:T(8,128)(2,1)} %latent_ref.1) | copy-start | bytes 110596
  0.9 16.4 %copy-start.3 = (s32[16]{0:T(128)S(1)}, s32[16]{0:T(128)}, u32[]{:S(2)}) copy-start(s32[16]{0:T(128)} %order_ref.1) | copy-start | bytes 196
  0.9 16.4 %copy-start.4 = (f32[512,128]{1,0:T(8,128)S(1)}, f32[512,128]{1,0:T(8,128)}, u32[]{:S(2)}) copy-start(f32[512,128]{1,0:T(8,128)} %constant.2.clone.table) | copy-start | bytes 786436
where the time goes:
time: 23.4 us; the launch traced here: 23.2 us
  Pallas kernels  22.3 us (95%)
  local copies, waits for them, and re-layouts  0.94 us (4%)
    pallas_call x1, Pallas kernels, per_device(): pl.pallas_call(functools.partial(gather_kernel, dims), out_shape=jax.Shap...  16.4 us
    pallas_call x1, Pallas kernels, per_device(): pl.pallas_call(functools.partial(attend_kernel, dims), out_shape=jax.Shap...  5.9 us
    unnamed x10, local copies, waits for them, and re-layouts  0.94 us

commit v1 on v0

--- a/solution.py
+++ b/solution.py
@@ -75,45 +75,42 @@
     p_recv,
     d_send,
     d_recv,
+    ready,
 ):
     n_seq, n_head, heads, rank, span_len, kv_count, spans_seq = dims
     s = lax.axis_index("seq")
     h = lax.axis_index("head")
-
-    def device(seq, head):
-        return {"seq": seq, "head": head}
-
-    hops = [1 << b for b in range(1, (n_seq - 1).bit_length())]
     far = range(2, n_seq, 2)
-
-    def last_hop(k, d):
-        bits = [b for b in hops if d & b]
-        return d
-
     mesh_id = pl.DeviceIdType.MESH
     barrier = pltpu.get_barrier_semaphore()
-    peers = [(s, flip(h, k)) for k in range(1, n_head)]
-    peers += [(flip(s, d), h) for d in far]
-    peers += [(flip(s, 1), h)]
-    for seq, head in peers:
-        pl.semaphore_signal(barrier, inc=1, device_id=device(seq, head), device_id_type=mesh_id)
-    kv[s * n_head + h] = latent_ref[...]
-    pl.semaphore_wait(barrier, len(peers))
+    peers = [(d, 0) for d in far] + [(0, k) for k in range(1, n_head)] + [(1, 0)]
+    peers.sort(key=lambda peer: bin(peer[0]).count("1") + (peer[1] + peer[1] // 2) * 0.9)
+
+    def signal(sem, d, k):
+        pl.semaphore_signal(
+            sem,
+            inc=1,
+            device_id={"seq": flip(s, d), "head": flip(h, k)},
+            device_id_type=mesh_id,
+        )
+
+    def later(d, k):
+        return flip(h, k) > h if k else flip(s, d) > s
 
     sent = []
 
-    def go(d, k, send, recv, seq, head):
+    def describe(d, k, send, recv, to_d, to_k):
         block = kv.at[flip(s, d) * n_head + flip(h, k)]
         copy = pltpu.make_async_remote_copy(
             src_ref=block if d or k else latent_ref,
             dst_ref=block,
             send_sem=send,
             recv_sem=recv,
-            device_id=device(seq, head),
+            device_id={"seq": flip(s, to_d), "head": flip(h, to_k)},
             device_id_type=mesh_id,
         )
-        copy.start()
         sent.append(copy)
+        return copy
 
     def arrived(d, k, send, recv):
         block = kv.at[flip(s, d) * n_head + flip(h, k)]
@@ -122,28 +119,69 @@
             dst_ref=block,
             send_sem=send,
             recv_sem=recv,
-            device_id=device(flip(s, 1), h),
+            device_id={"seq": flip(s, 1), "head": h},
             device_id_type=mesh_id,
         ).wait_recv()
 
+    before = jnp.int32(0)
+    for peer in peers:
+        before = before + jnp.where(later(*peer), 0, 1)
+
+        @pl.when(later(*peer))
+        def _(peer=peer):
+            signal(barrier, *peer)
+
+    kv[s * n_head + h] = latent_ref[...]
+
+    @pl.when(before > 0)
+    def _():
+        pl.semaphore_wait(barrier, before)
+
+    for i, peer in enumerate(peers):
+
+        @pl.when(jnp.logical_not(later(*peer)))
+        def _(i=i, peer=peer):
+            signal(ready.at[i], *peer)
+
+    first = []
+    for d, k in peers:
+        if k:
+            first.append(describe(0, 0, z_send.at[k - 1], z_recv.at[k - 1], 0, k))
+        elif d > 1:
+            first.append(describe(0, 0, p_send.at[0, d // 2], p_recv.at[0, d // 2], d, 0))
+        else:
+            first.append(describe(0, 0, d_send.at[0, 0], d_recv.at[0, 0], 1, 0))
+    for peer, copy in zip(peers, first):
+        pl.when(jnp.logical_not(later(*peer)))(copy.start)
+    for i, (peer, copy) in enumerate(zip(peers, first)):
+
+        @pl.when(later(*peer))
+        def _(i=i, copy=copy):
+            pl.semaphore_wait(ready.at[i], 1)
+            copy.start()
+
     def spread(k, d):
-        for to in reversed(far):
-            hop = last_hop(k, to)
-            if to - hop == d:
-                go(d, k, p_send.at[k, to // 2], p_recv.at[k, to // 2], flip(s, hop), h)
-        go(d, k, d_send.at[k, d // 2], d_recv.at[k, d // 2], flip(s, 1), h)
-
-    for k in range(1, n_head):
-        go(0, 0, z_send.at[k - 1], z_recv.at[k - 1], s, flip(h, k))
-    events = [((k + bin(d).count("1") + 2) if d else k, d, k) for k in range(n_head) for d in range(0, n_seq, 2)]
+        if d == 0:
+            for to in reversed(far):
+                describe(0, k, p_send.at[k, to // 2], p_recv.at[k, to // 2], to, 0).start()
+        describe(d, k, d_send.at[k, d // 2], d_recv.at[k, d // 2], 1, 0).start()
+
+    events = []
+    for k in range(n_head):
+        for d in range(0, n_seq, 2):
+            if d:
+                events.append((k + bin(d).count("1") + 2, d, k))
+            elif k:
+                events.append((k, d, k))
     for _, d, k in sorted(events):
         if d:
             arrived(d, k, p_send.at[k, d // 2], p_recv.at[k, d // 2])
-        elif k:
+        else:
             arrived(0, k, z_send.at[k - 1], z_recv.at[k - 1])
         spread(k, d)
-    for _, d, k in sorted(events):
-        arrived(d + 1, k, d_send.at[k, d // 2], d_recv.at[k, d // 2])
+    for k in range(n_head):
+        for d in range(0, n_seq, 2):
+            arrived(d + 1, k, d_send.at[k, d // 2], d_recv.at[k, d // 2])
     for copy in sent:
         copy.wait_send()
 
@@ -295,6 +333,7 @@
             dma((n_head, n_seq // 2)),
             dma((n_head, n_seq // 2)),
             dma((n_head, n_seq // 2)),
+            pltpu.SemaphoreType.REGULAR((n_head + n_seq // 2 - 1,)),
         ],
         compiler_params=pltpu.CompilerParams(
             collective_id=0, has_side_effects=True, vmem_limit_bytes=GATHER_MIB << 20

time: 23.4 us -> 22.1 us (0.944)
  Pallas kernels: 22.3 us -> 21 us
    pallas_call x1, Pallas kernels: 16.4 us -> 15.1 us  [per_device(): pl.pallas_call(functools.partial(gather_kernel, dims), out_shape=jax.Shap...]
where the time goes in v1:
time: 22.1 us; the launch traced here: 21.9 us
  Pallas kernels  21 us (95%)
  local copies, waits for them, and re-layouts  0.94 us (4%)
    pallas_call x1, Pallas kernels, per_device(): pl.pallas_call(functools.partial(gather_kernel, dims), out_shape=jax.Shap...  15.1 us
    pallas_call x1, Pallas kernels, per_device(): pl.pallas_call(functools.partial(attend_kernel, dims), out_shape=jax.Shap...  5.9 us
    unnamed x10, local copies, waits for them, and re-layouts  0.94 us

profile of v1, /device:TPU:0, one launch (start us, length us, event | category | flops | bytes accessed | tf_op | source)
XLA Modules:
  0.0 21.9 jit_solution(6568572504211384613)
XLA Ops:
  0.0 0.0 copy-start.1
  0.0 0.0 copy-start
  0.0 0.0 copy-start.2
  0.0 0.9 %copy-done.2 = bf16[32,576]{1,0:T(8,128)(2,1)S(1)} copy-done((bf16[32,576]{1,0:T(8,128)(2,1)S(1)}, bf16[32,576]{1,0:T(8,128)(2,1)}, u32[]{:S(2)}) %copy-start.2) | copy-done | bytes 36888
  0.9 0.0 copy-start.3
  0.9 0.0 copy-start.4
  0.9 15.1 %gather_keys.1.kv = bf16[32,32,576]{2,1,0:T(8,128)(2,1)S(1)} custom-call(bf16[32,576]{1,0:T(8,128)(2,1)S(1)} %copy-done.2), custom_call_target="tpu_custom_call" | custom-call | flops 21474836480 | bytes 1048576 | tf_op jit(solution)/shard_map/gather_keys/pallas_call | solution.py:324
  16.0 0.0 copy-done.1
  16.0 0.0 copy-done
  16.0 0.0 copy-done.3
  16.0 0.0 copy-done.4
  16.0 5.9 %attend.1 = bf16[128,2048]{1,0:T(8,128)(2,1)} custom-call(s32[16]{0:T(128)S(1)} %copy-done.3, bf16[128,9216]{1,0:T(8,128)(2,1)S(1)} %copy-done, bf16[32,32,576]{2,1,0:T(8,128)(2,1)S(1)} %gather_keys.1.kv, f32[512,128]{1,0:T(8,128)S(1)} %copy-done.4, bf16[16,512,128]{2,1,0:T(8,128)(2,1)S(1)} %copy-done.1), custom_call_target="tpu_custom_call" | custom-call | flops 4294967296 | bytes 8388608 | tf_op jit(solution)/shard_map/attend/pallas_call | solution.py:344
Async XLA Ops:
  0.0 16.0 %copy-start.1 = (bf16[16,512,128]{2,1,0:T(8,128)(2,1)S(1)}, bf16[16,512,128]{2,1,0:T(8,128)(2,1)}, u32[]{:S(2)}) copy-start(bf16[16,512,128]{2,1,0:T(8,128)(2,1)} %w_ref.1) | copy-start | bytes 6291460
  0.0 16.0 %copy-start = (bf16[128,9216]{1,0:T(8,128)(2,1)S(1)}, bf16[128,9216]{1,0:T(8,128)(2,1)}, u32[]{:S(2)}) copy-start(bf16[128,9216]{1,0:T(8,128)(2,1)} %queries_ref.1) | copy-start | bytes 7077892
  0.0 0.9 %copy-start.2 = (bf16[32,576]{1,0:T(8,128)(2,1)S(1)}, bf16[32,576]{1,0:T(8,128)(2,1)}, u32[]{:S(2)}) copy-start(bf16[32,576]{1,0:T(8,128)(2,1)} %latent_ref.1) | copy-start | bytes 110596
  0.9 15.1 %copy-start.3 = (s32[16]{0:T(128)S(1)}, s32[16]{0:T(128)}, u32[]{:S(2)}) copy-start(s32[16]{0:T(128)} %order_ref.1) | copy-start | bytes 196
  0.9 15.1 %copy-start.4 = (f32[512,128]{1,0:T(8,128)S(1)}, f32[512,128]{1,0:T(8,128)}, u32[]{:S(2)}) copy-start(f32[512,128]{1,0:T(8,128)} %constant.2.clone.table) | copy-start | bytes 786436

commit v2 on v1

--- a/solution.py
+++ b/solution.py
@@ -14,11 +14,14 @@
 SEQS = 2
 LANES = 128
 CHUNK_SPANS = 8
+PARTS = 1
+PUTS = 4
 GATHER_MIB = 24
 ATTEND_MIB = 40
 
 theta_base = 10000.0
 logit_scale = (NOPE_DIM + ROPE_DIM) ** -0.5
+exponent_scale = logit_scale * math.log2(math.e)
 
 
 def angle_table(count, half):
@@ -187,7 +190,7 @@
 
 
 def attend_kernel(
-    dims, order_ref, queries_ref, kv, table, w_ref, out_ref, q_rows, keys, mixed, state
+    dims, order_hbm, queries_ref, kv, table, w_ref, out_ref, q_rows, keys, mixed, state, result, put_sem, order_ref, order_sem
 ):
     n_seq, n_head, heads, rank, span_len, kv_count, spans_seq = dims
     width = rank + ROPE_DIM
@@ -195,21 +198,27 @@
     s = lax.axis_index("seq")
     spans = SEQS * spans_seq
     per_span = span_len // kv_count
-    seq_first, place = span_places(order_ref, s, spans_seq, span_len)
-    for span in range(2):
-        angles = table[pl.ds(place[span], span_len), :]
+    rows_all = heads * span_len
+    order = pltpu.make_async_copy(order_hbm, order_ref, order_sem)
+    order.start()
+
+    def copy_queries(span):
         for par in range(2):
             for pair in range(pairs):
                 source = pl.ds(span * span_len, span_len)
                 first = pair * 2 * width + par * rank
-                rows = pl.ds(pair * span_len, span_len)
-                tiles = [
-                    queries_ref[source, pl.ds(first + c, LANES)] for c in range(0, rank + 1, LANES)
-                ]
-                tiles[-1] = rotate_tile(
-                    tiles[-1].astype(jnp.float32), angles, bool(par)
-                ).astype(jnp.bfloat16)
-                q_rows[span, par, rows, :] = jnp.concatenate(tiles, 1)
+                rows = pl.ds((pair * 2 + par) * span_len, span_len)
+                whole = queries_ref[source, pl.ds(first, rank + LANES)]
+                if par:
+                    whole = pltpu.roll(whole, rank + LANES - ROPE_DIM, 1)
+                q_rows[span, rows, :] = whole
+
+    def rotate_queries(span):
+        angles = table[pl.ds(place[span], span_len), :]
+        for head in range(heads):
+            rows = pl.ds(head * span_len, span_len)
+            tail = q_rows[span, rows, rank:].astype(jnp.float32)
+            q_rows[span, rows, rank:] = rotate_tile(tail, angles, False).astype(jnp.bfloat16)
 
     def block_of(stream_span):
         def pick(slot, found):
@@ -226,82 +235,95 @@
     n_chunks = spans_seq // chunk_spans
     chunk = chunk_spans * span_len
 
-    for span in range(2):
-        def one_chunk(c, span=span):
-            for j in range(chunk_spans):
-                block = block_of(seq_first[span] + c * chunk_spans + j)
-                raw = kv[pl.ds(block, per_span)].reshape(span_len, width)
-                angles = table[pl.ds((c * chunk_spans + j) * span_len, span_len), :]
-                pad = jnp.zeros((span_len, LANES - ROPE_DIM), jnp.float32)
-                rope = jnp.concatenate([raw[:, rank:].astype(jnp.float32), pad], 1)
-                rope = rotate_tile(rope, angles, False)
-                rows = pl.ds(j * span_len, span_len)
-                keys[0, rows, :rank] = raw[:, :rank]
-                keys[0, rows, rank:] = rope.astype(jnp.bfloat16)
-                whole = jnp.concatenate([raw[:, :rank].astype(jnp.float32), rope], 1)
-                keys[1, rows, :] = pltpu.roll(whole, ROPE_DIM, 1).astype(jnp.bfloat16)
-            limit = lax.broadcasted_iota(jnp.int32, (span_len, chunk), 0) + place[span]
-            seen = lax.broadcasted_iota(jnp.int32, (span_len, chunk), 1) + c * chunk <= limit
-            for par in range(2):
-                scores = (
-                    lax.dot_general(
-                        q_rows[span, par],
-                        keys[par],
-                        (((1,), (1,)), ((), ())),
-                        preferred_element_type=jnp.float32,
-                    )
-                    * logit_scale
-                )
-                scores = jnp.where(
-                    seen[None], scores.reshape(pairs, span_len, chunk), -jnp.inf
-                ).reshape(pairs * span_len, chunk)
-                top = jnp.max(scores, 1, keepdims=True)
-                if n_chunks > 1:
-                    old_top = state[par, :, 0:1]
-                    top = jnp.maximum(top, old_top)
-                    shrink = jnp.exp(old_top - top)
-                expo = jnp.exp(scores - top)
-                total = jnp.sum(expo, 1, keepdims=True)
-                sums = jnp.dot(
-                    expo.astype(jnp.bfloat16),
-                    keys[0, :, :rank],
+    def prepare_keys(span, c):
+        for j in range(chunk_spans):
+            block = block_of(seq_first[span] + c * chunk_spans + j)
+            raw = kv[pl.ds(block, per_span)].reshape(span_len, width)
+            angles = table[pl.ds((c * chunk_spans + j) * span_len, span_len), :]
+            pad = jnp.zeros((span_len, LANES - ROPE_DIM), jnp.float32)
+            rope = jnp.concatenate([raw[:, rank:].astype(jnp.float32), pad], 1)
+            rows = pl.ds(j * span_len, span_len)
+            keys[span, rows, :rank] = raw[:, :rank]
+            keys[span, rows, rank:] = rotate_tile(rope, angles, False).astype(jnp.bfloat16)
+
+    def one_chunk(span, c):
+        limit = lax.broadcasted_iota(jnp.int32, (span_len, chunk), 0) + place[span]
+        seen = lax.broadcasted_iota(jnp.int32, (span_len, chunk), 1) + c * chunk <= limit
+        for part in range(PARTS):
+            share = heads // PARTS
+            rows = pl.ds(part * share * span_len, share * span_len)
+            scores = (
+                lax.dot_general(
+                    q_rows[span, rows, :],
+                    keys[span],
+                    (((1,), (1,)), ((), ())),
                     preferred_element_type=jnp.float32,
                 )
-                if n_chunks > 1:
-                    total = state[par, :, LANES : LANES + 1] * shrink + total
-                    sums = state[par, :, 2 * LANES :] * shrink + sums
-                    state[par, :, :LANES] = jnp.broadcast_to(top, (pairs * span_len, LANES))
-                    state[par, :, LANES : 2 * LANES] = jnp.broadcast_to(
-                        total, (pairs * span_len, LANES)
-                    )
-                    state[par, :, 2 * LANES :] = sums
-                else:
-                    finish(par, sums, total)
-
-        def finish(par, sums, total, span=span):
-            result = (sums / total).astype(jnp.bfloat16)
-            mixed[par, :, pl.ds(span * span_len, span_len), :] = result.reshape(
-                pairs, span_len, rank
+                * exponent_scale
             )
-
+            scores = jnp.where(
+                seen[None], scores.reshape(share, span_len, chunk), -jnp.inf
+            ).reshape(share * span_len, chunk)
+            top = jnp.max(scores, 1, keepdims=True)
+            if n_chunks > 1:
+                old_top = state[rows, 0:1]
+                top = jnp.maximum(top, old_top)
+                shrink = jnp.exp2(old_top - top)
+            expo = jnp.exp2(scores - top)
+            total = jnp.sum(expo, 1, keepdims=True)
+            sums = jnp.dot(
+                expo.astype(jnp.bfloat16),
+                keys[span, :, :rank],
+                preferred_element_type=jnp.float32,
+            )
+            if n_chunks > 1:
+                total = state[rows, LANES : LANES + 1] * shrink + total
+                sums = state[rows, 2 * LANES :] * shrink + sums
+                state[rows, :LANES] = jnp.broadcast_to(top, (share * span_len, LANES))
+                state[rows, LANES : 2 * LANES] = jnp.broadcast_to(total, (share * span_len, LANES))
+                state[rows, 2 * LANES :] = sums
+            else:
+                finish(span, part * share, share, sums, total)
+
+    def finish(span, first, count, sums, total):
+        result = (sums * (1.0 / total)).astype(jnp.bfloat16)
+        mixed[pl.ds(first, count), pl.ds(span * span_len, span_len), :] = result.reshape(
+            count, span_len, rank
+        )
+
+    for span in range(2):
+        copy_queries(span)
+    order.wait()
+    seq_first, place = span_places(order_ref, s, spans_seq, span_len)
+    for span in range(2):
+        rotate_queries(span)
         if n_chunks == 1:
-            one_chunk(0)
+            prepare_keys(span, 0)
+            one_chunk(span, 0)
         else:
-            state[:, :, :LANES] = jnp.full((2, pairs * span_len, LANES), -1e30, jnp.float32)
-            state[:, :, LANES:] = jnp.zeros((2, pairs * span_len, LANES + rank), jnp.float32)
+            state[:, :LANES] = jnp.full((rows_all, LANES), -1e30, jnp.float32)
+            state[:, LANES:] = jnp.zeros((rows_all, LANES + rank), jnp.float32)
 
             @pl.loop(0, n_chunks)
-            def _(c):
-                one_chunk(c)
-
-            for par in range(2):
-                finish(par, state[par, :, 2 * LANES :], state[par, :, LANES : LANES + 1])
+            def _(c, span=span):
+                prepare_keys(span, c)
+                one_chunk(span, c)
+
+            finish(span, 0, heads, state[:, 2 * LANES :], state[:, LANES : LANES + 1])
 
     v_dim = w_ref.shape[2]
-    for head in range(heads):
-        out_ref[:, pl.ds(head * v_dim, v_dim)] = jnp.dot(
-            mixed[head % 2, head // 2], w_ref[head], preferred_element_type=jnp.float32
-        ).astype(jnp.bfloat16)
+    puts = []
+    for part in range(PUTS):
+        share = heads // PUTS
+        for head in range(part * share, part * share + share):
+            result[:, pl.ds(head * v_dim, v_dim)] = jnp.dot(
+                mixed[head], w_ref[head], preferred_element_type=jnp.float32
+            ).astype(jnp.bfloat16)
+        lanes = pl.ds(part * share * v_dim, share * v_dim)
+        puts.append(pltpu.make_async_copy(result.at[:, lanes], out_ref.at[:, lanes], put_sem.at[part]))
+        puts[-1].start()
+    for put in puts:
+        put.wait()
 
 
 def per_device(n_seq, n_head, span_order, queries, latent_kv, w_uv):
@@ -312,14 +334,12 @@
     spans = span_order.shape[0]
     spans_seq = spans // SEQS
     seq_len = spans_seq * span_len
-    pairs = heads // 2
     wide = rank + LANES
     chunk_spans = min(CHUNK_SPANS, spans_seq)
-    state_rows = pairs * span_len if spans_seq > chunk_spans else 8
+    state_rows = heads * span_len if spans_seq > chunk_spans else 8
     dims = (n_seq, n_head, heads, rank, span_len, kv_count, spans_seq)
     table = jnp.asarray(angle_table(seq_len, ROPE_DIM // 2))
     dma = pltpu.SemaphoreType.DMA
-    smem = pl.BlockSpec(memory_space=pltpu.SMEM)
     vmem = pl.BlockSpec(memory_space=pltpu.VMEM)
     kv = pl.pallas_call(
         functools.partial(gather_kernel, dims),
@@ -344,13 +364,17 @@
     return pl.pallas_call(
         functools.partial(attend_kernel, dims),
         out_shape=jax.ShapeDtypeStruct((tok_dev, heads * v_dim), jnp.bfloat16),
-        in_specs=[smem, vmem, vmem, vmem, vmem],
-        out_specs=vmem,
+        in_specs=[pl.BlockSpec(memory_space=pl.ANY), vmem, vmem, vmem, vmem],
+        out_specs=pl.BlockSpec(memory_space=pl.ANY),
         scratch_shapes=[
-            pltpu.VMEM((2, 2, pairs * span_len, wide), jnp.bfloat16),
+            pltpu.VMEM((2, heads * span_len, wide), jnp.bfloat16),
             pltpu.VMEM((2, chunk_spans * span_len, wide), jnp.bfloat16),
-            pltpu.VMEM((2, pairs, tok_dev, rank), jnp.bfloat16),
-            pltpu.VMEM((2, state_rows, 2 * LANES + rank), jnp.float32),
+            pltpu.VMEM((heads, tok_dev, rank), jnp.bfloat16),
+            pltpu.VMEM((state_rows, 2 * LANES + rank), jnp.float32),
+            pltpu.VMEM((tok_dev, heads * v_dim), jnp.bfloat16),
+            dma((PUTS,)),
+            pltpu.SMEM(span_order.shape, jnp.int32),
+            dma,
         ],
         compiler_params=pltpu.CompilerParams(vmem_limit_bytes=ATTEND_MIB << 20),
         cost_estimate=pl.CostEstimate(flops=4 << 30, bytes_accessed=8 << 20, transcendentals=1 << 20),

time: 22.1 us -> 21.3 us (0.964)
  Pallas kernels: 21 us -> 20.1 us
    pallas_call x1, Pallas kernels: 5.9 us -> 5.09 us  [per_device(): pl.pallas_call(functools.partial(attend_kernel, dims), out_shape=jax.Shap...]
where the time goes in v2:
time: 21.3 us; the launch traced here: 21.1 us
  Pallas kernels  20.1 us (94%)
  local copies, waits for them, and re-layouts  0.94 us (4%)
    pallas_call x1, Pallas kernels, per_device(): pl.pallas_call(functools.partial(gather_kernel, dims), out_shape=jax.Shap...  15.1 us
    pallas_call x1, Pallas kernels, per_device(): pl.pallas_call(functools.partial(attend_kernel, dims), out_shape=jax.Shap...  5.09 us
    unnamed x10, local copies, waits for them, and re-layouts  0.94 us

profile of v2, /device:TPU:0, one launch (start us, length us, event | category | flops | bytes accessed | tf_op | source)
XLA Modules:
  0.0 21.1 jit_solution(1050813026123141175)
XLA Ops:
  0.0 0.0 copy-start.1
  0.0 0.0 copy-start
  0.0 0.0 copy-start.2
  0.0 0.9 %copy-done.2 = bf16[32,576]{1,0:T(8,128)(2,1)S(1)} copy-done((bf16[32,576]{1,0:T(8,128)(2,1)S(1)}, bf16[32,576]{1,0:T(8,128)(2,1)}, u32[]{:S(2)}) %copy-start.2) | copy-done | bytes 36888
  0.9 0.0 copy-start.3
  0.9 0.0 copy-start.4
  0.9 15.1 %gather_keys.1.kv = bf16[32,32,576]{2,1,0:T(8,128)(2,1)S(1)} custom-call(bf16[32,576]{1,0:T(8,128)(2,1)S(1)} %copy-done.2), custom_call_target="tpu_custom_call" | custom-call | flops 21474836480 | bytes 1048576 | tf_op jit(solution)/shard_map/gather_keys/pallas_call | solution.py:344
  16.0 0.0 copy-done.1
  16.0 0.0 copy-done
  16.0 0.0 copy-done.3
  16.0 0.0 copy-done.4
  16.0 5.1 %attend.1 = bf16[128,2048]{1,0:T(8,128)(2,1)} custom-call(s32[16]{0:T(128)S(1)} %copy-done.3, bf16[128,9216]{1,0:T(8,128)(2,1)S(1)} %copy-done, bf16[32,32,576]{2,1,0:T(8,128)(2,1)S(1)} %gather_keys.1.kv, f32[512,128]{1,0:T(8,128)S(1)} %copy-done.4, bf16[16,512,128]{2,1,0:T(8,128)(2,1)S(1)} %copy-done.1), custom_call_target="tpu_custom_call" | custom-call | flops 4294967296 | bytes 8388608 | tf_op jit(solution)/shard_map/attend/pallas_call | solution.py:364
Async XLA Ops:
  0.0 16.0 %copy-start.1 = (bf16[16,512,128]{2,1,0:T(8,128)(2,1)S(1)}, bf16[16,512,128]{2,1,0:T(8,128)(2,1)}, u32[]{:S(2)}) copy-start(bf16[16,512,128]{2,1,0:T(8,128)(2,1)} %w_ref.1) | copy-start | bytes 6291460
  0.0 16.0 %copy-start = (bf16[128,9216]{1,0:T(8,128)(2,1)S(1)}, bf16[128,9216]{1,0:T(8,128)(2,1)}, u32[]{:S(2)}) copy-start(bf16[128,9216]{1,0:T(8,128)(2,1)} %queries_ref.1) | copy-start | bytes 7077892
  0.0 0.9 %copy-start.2 = (bf16[32,576]{1,0:T(8,128)(2,1)S(1)}, bf16[32,576]{1,0:T(8,128)(2,1)}, u32[]{:S(2)}) copy-start(bf16[32,576]{1,0:T(8,128)(2,1)} %latent_ref.1) | copy-start | bytes 110596
  0.9 15.1 %copy-start.3 = (s32[16]{0:T(128)S(1)}, s32[16]{0:T(128)}, u32[]{:S(2)}) copy-start(s32[16]{0:T(128)} %order_hbm.1) | copy-start | bytes 196
  0.9 15.1 %copy-start.4 = (f32[512,128]{1,0:T(8,128)S(1)}, f32[512,128]{1,0:T(8,128)}, u32[]{:S(2)}) copy-start(f32[512,128]{1,0:T(8,128)} %constant.2.clone.table) | copy-start | bytes 786436

commit v3 on v2

--- a/solution.py
+++ b/solution.py
@@ -105,7 +105,7 @@
     def describe(d, k, send, recv, to_d, to_k):
         block = kv.at[flip(s, d) * n_head + flip(h, k)]
         copy = pltpu.make_async_remote_copy(
-            src_ref=block if d or k else latent_ref,
+            src_ref=block,
             dst_ref=block,
             send_sem=send,
             recv_sem=recv,
@@ -126,6 +126,16 @@
             device_id_type=mesh_id,
         ).wait_recv()
 
+    mine = s * n_head + h
+    for c in range(0, rank, LANES):
+        kv[mine, pl.ds(c // LANES * kv_count, kv_count), :] = latent_ref[:, pl.ds(c, LANES)]
+    tail = latent_ref[:, rank:].astype(jnp.float32)
+    tail = jnp.concatenate([tail, jnp.zeros((kv_count, LANES - ROPE_DIM), jnp.float32)], 1)
+    low, high = tail[: kv_count // 2], tail[kv_count // 2 :]
+    kv[mine, pl.ds(rank // LANES * kv_count, kv_count // 2), :] = (
+        low + pltpu.roll(high, ROPE_DIM, 1)
+    ).astype(jnp.bfloat16)
+
     before = jnp.int32(0)
     for peer in peers:
         before = before + jnp.where(later(*peer), 0, 1)
@@ -134,7 +144,6 @@
         def _(peer=peer):
             signal(barrier, *peer)
 
-    kv[s * n_head + h] = latent_ref[...]
 
     @pl.when(before > 0)
     def _():
@@ -155,13 +164,27 @@
         else:
             first.append(describe(0, 0, d_send.at[0, 0], d_recv.at[0, 0], 1, 0))
     for peer, copy in zip(peers, first):
-        pl.when(jnp.logical_not(later(*peer)))(copy.start)
-    for i, (peer, copy) in enumerate(zip(peers, first)):
-
-        @pl.when(later(*peer))
-        def _(i=i, copy=copy):
-            pl.semaphore_wait(ready.at[i], 1)
-            copy.start()
+        near = flip(h, peer[1]) != 0
+        pl.when(jnp.logical_not(later(*peer)) & jnp.logical_not(near))(copy.start)
+    for peer, copy in zip(peers, first):
+        near = flip(h, peer[1]) != 0
+        pl.when(jnp.logical_not(later(*peer)) & near)(copy.start)
+    def send_later(chosen):
+        for i, (peer, copy) in enumerate(zip(peers, first)):
+            distant = flip(h, peer[1]) - h >= n_head - 1
+            if peer[1]:
+                due = later(*peer) & (distant == chosen)
+            elif chosen:
+                continue
+            else:
+                due = later(*peer)
+
+            @pl.when(due)
+            def _(i=i, copy=copy):
+                pl.semaphore_wait(ready.at[i], 1)
+                copy.start()
+
+    send_later(False)
 
     def spread(k, d):
         if d == 0:
@@ -173,10 +196,12 @@
     for k in range(n_head):
         for d in range(0, n_seq, 2):
             if d:
-                events.append((k + bin(d).count("1") + 2, d, k))
+                events.append((k + 3 + (bin(d).count("1") - 1) * 0.05, d, k))
             elif k:
                 events.append((k, d, k))
-    for _, d, k in sorted(events):
+    for turn, (_, d, k) in enumerate(sorted(events)):
+        if turn == 1:
+            send_later(True)
         if d:
             arrived(d, k, p_send.at[k, d // 2], p_recv.at[k, d // 2])
         else:
@@ -238,13 +263,21 @@
     def prepare_keys(span, c):
         for j in range(chunk_spans):
             block = block_of(seq_first[span] + c * chunk_spans + j)
-            raw = kv[pl.ds(block, per_span)].reshape(span_len, width)
             angles = table[pl.ds((c * chunk_spans + j) * span_len, span_len), :]
-            pad = jnp.zeros((span_len, LANES - ROPE_DIM), jnp.float32)
-            rope = jnp.concatenate([raw[:, rank:].astype(jnp.float32), pad], 1)
+            rope = []
+            for piece in range(per_span):
+                rows = pl.ds(j * span_len + piece * kv_count, kv_count)
+                for t in range(rank // LANES):
+                    keys[span, rows, pl.ds(t * LANES, LANES)] = kv[
+                        block + piece, pl.ds(t * kv_count, kv_count), :
+                    ]
+                tail = kv[block + piece, pl.ds(rank // LANES * kv_count, kv_count // 2), :]
+                tail = tail.astype(jnp.float32)
+                rope += [tail, pltpu.roll(tail, LANES - ROPE_DIM, 1)]
+            rope = rotate_tile(jnp.concatenate(rope, 0), angles, False)
+            lane = lax.broadcasted_iota(jnp.int32, rope.shape, 1)
             rows = pl.ds(j * span_len, span_len)
-            keys[span, rows, :rank] = raw[:, :rank]
-            keys[span, rows, rank:] = rotate_tile(rope, angles, False).astype(jnp.bfloat16)
+            keys[span, rows, rank:] = jnp.where(lane < ROPE_DIM, rope, 0.0).astype(jnp.bfloat16)
 
     def one_chunk(span, c):
         limit = lax.broadcasted_iota(jnp.int32, (span_len, chunk), 0) + place[span]
@@ -335,6 +368,7 @@
     spans_seq = spans // SEQS
     seq_len = spans_seq * span_len
     wide = rank + LANES
+    packed = kv_count * width // LANES
     chunk_spans = min(CHUNK_SPANS, spans_seq)
     state_rows = heads * span_len if spans_seq > chunk_spans else 8
     dims = (n_seq, n_head, heads, rank, span_len, kv_count, spans_seq)
@@ -343,7 +377,7 @@
     vmem = pl.BlockSpec(memory_space=pltpu.VMEM)
     kv = pl.pallas_call(
         functools.partial(gather_kernel, dims),
-        out_shape=jax.ShapeDtypeStruct((n_seq * n_head, kv_count, width), jnp.bfloat16),
+        out_shape=jax.ShapeDtypeStruct((n_seq * n_head, packed, LANES), jnp.bfloat16),
         in_specs=[vmem],
         out_specs=vmem,
         scratch_shapes=[

time: 21.3 us -> 20.9 us (0.981)
  Pallas kernels: 20.1 us -> 19.6 us
    pallas_call x1, Pallas kernels: 15.1 us -> 14.4 us  [per_device(): pl.pallas_call(functools.partial(gather_kernel, dims), out_shape=jax.Shap...]
where the time goes in v3:
time: 20.9 us; the launch traced here: 20.6 us
  Pallas kernels  19.6 us (94%)
  local copies, waits for them, and re-layouts  0.94 us (4%)
    pallas_call x1, Pallas kernels, per_device(): pl.pallas_call(functools.partial(gather_kernel, dims), out_shape=jax.Shap...  14.4 us
    pallas_call x1, Pallas kernels, per_device(): pl.pallas_call(functools.partial(attend_kernel, dims), out_shape=jax.Shap...  5.2 us
    unnamed x10, local copies, waits for them, and re-layouts  0.94 us

profile of v3, /device:TPU:0, one launch (start us, length us, event | category | flops | bytes accessed | tf_op | source)
XLA Modules:
  0.0 20.6 jit_solution(5324149073202724695)
XLA Ops:
  0.0 0.0 copy-start.1
  0.0 0.0 copy-start
  0.0 0.0 copy-start.2
  0.0 0.9 %copy-done.2 = bf16[32,576]{1,0:T(8,128)(2,1)S(1)} copy-done((bf16[32,576]{1,0:T(8,128)(2,1)S(1)}, bf16[32,576]{1,0:T(8,128)(2,1)}, u32[]{:S(2)}) %copy-start.2) | copy-done | bytes 36888
  0.9 0.0 copy-start.3
  0.9 0.0 copy-start.4
  0.9 14.4 %gather_keys.1.kv = bf16[32,144,128]{2,1,0:T(8,128)(2,1)S(1)} custom-call(bf16[32,576]{1,0:T(8,128)(2,1)S(1)} %copy-done.2), custom_call_target="tpu_custom_call" | custom-call | flops 21474836480 | bytes 1048576 | tf_op jit(solution)/shard_map/gather_keys/pallas_call | solution.py:378
  15.3 0.0 copy-done.1
  15.3 0.0 copy-done
  15.3 0.0 copy-done.3
  15.3 0.0 copy-done.4
  15.3 5.2 %attend.1 = bf16[128,2048]{1,0:T(8,128)(2,1)} custom-call(s32[16]{0:T(128)S(1)} %copy-done.3, bf16[128,9216]{1,0:T(8,128)(2,1)S(1)} %copy-done, bf16[32,144,128]{2,1,0:T(8,128)(2,1)S(1)} %gather_keys.1.kv, f32[512,128]{1,0:T(8,128)S(1)} %copy-done.4, bf16[16,512,128]{2,1,0:T(8,128)(2,1)S(1)} %copy-done.1), custom_call_target="tpu_custom_call" | custom-call | flops 4294967296 | bytes 8388608 | tf_op jit(solution)/shard_map/attend/pallas_call | solution.py:398
Async XLA Ops:
  0.0 15.3 %copy-start.1 = (bf16[16,512,128]{2,1,0:T(8,128)(2,1)S(1)}, bf16[16,512,128]{2,1,0:T(8,128)(2,1)}, u32[]{:S(2)}) copy-start(bf16[16,512,128]{2,1,0:T(8,128)(2,1)} %w_ref.1) | copy-start | bytes 6291460
  0.0 15.3 %copy-start = (bf16[128,9216]{1,0:T(8,128)(2,1)S(1)}, bf16[128,9216]{1,0:T(8,128)(2,1)}, u32[]{:S(2)}) copy-start(bf16[128,9216]{1,0:T(8,128)(2,1)} %queries_ref.1) | copy-start | bytes 7077892
  0.0 0.9 %copy-start.2 = (bf16[32,576]{1,0:T(8,128)(2,1)S(1)}, bf16[32,576]{1,0:T(8,128)(2,1)}, u32[]{:S(2)}) copy-start(bf16[32,576]{1,0:T(8,128)(2,1)} %latent_ref.1) | copy-start | bytes 110596
  0.9 14.4 %copy-start.3 = (s32[16]{0:T(128)S(1)}, s32[16]{0:T(128)}, u32[]{:S(2)}) copy-start(s32[16]{0:T(128)} %order_hbm.1) | copy-start | bytes 196
  0.9 14.4 %copy-start.4 = (f32[512,128]{1,0:T(8,128)S(1)}, f32[512,128]{1,0:T(8,128)}, u32[]{:S(2)}) copy-start(f32[512,128]{1,0:T(8,128)} %constant.2.clone.table) | copy-start | bytes 786436

commit v4 on v3

--- a/solution.py
+++ b/solution.py
@@ -98,6 +98,8 @@
         )
 
     def later(d, k):
+        if d == 1:
+            return s % 2 == 1
         return flip(h, k) > h if k else flip(s, d) > s
 
     sent = []

time: 20.9 us -> 20.7 us (level); the launches traced: 20.6 us -> 20.6 us
  no operation moved by 1% of the time
where the time goes in v4:
time: 20.7 us; the launch traced here: 20.6 us
  Pallas kernels  19.6 us (95%)
  local copies, waits for them, and re-layouts  0.94 us (5%)
    pallas_call x1, Pallas kernels, per_device(): pl.pallas_call(functools.partial(gather_kernel, dims), out_shape=jax.Shap...  14.4 us
    pallas_call x1, Pallas kernels, per_device(): pl.pallas_call(functools.partial(attend_kernel, dims), out_shape=jax.Shap...  5.2 us
    unnamed x10, local copies, waits for them, and re-layouts  0.94 us

profile of v4, /device:TPU:0, one launch (start us, length us, event | category | flops | bytes accessed | tf_op | source)
XLA Modules:
  0.0 20.6 jit_solution(16719156114383862450)
XLA Ops:
  0.0 0.0 copy-start.1
  0.0 0.0 copy-start
  0.0 0.0 copy-start.2
  0.0 0.9 %copy-done.2 = bf16[32,576]{1,0:T(8,128)(2,1)S(1)} copy-done((bf16[32,576]{1,0:T(8,128)(2,1)S(1)}, bf16[32,576]{1,0:T(8,128)(2,1)}, u32[]{:S(2)}) %copy-start.2) | copy-done | bytes 36888
  0.9 0.0 copy-start.3
  0.9 0.0 copy-start.4
  0.9 14.4 %gather_keys.1.kv = bf16[32,144,128]{2,1,0:T(8,128)(2,1)S(1)} custom-call(bf16[32,576]{1,0:T(8,128)(2,1)S(1)} %copy-done.2), custom_call_target="tpu_custom_call" | custom-call | flops 21474836480 | bytes 1048576 | tf_op jit(solution)/shard_map/gather_keys/pallas_call | solution.py:380
  15.3 0.0 copy-done.1
  15.3 0.0 copy-done
  15.3 0.0 copy-done.3
  15.4 0.0 copy-done.4
  15.4 5.2 %attend.1 = bf16[128,2048]{1,0:T(8,128)(2,1)} custom-call(s32[16]{0:T(128)S(1)} %copy-done.3, bf16[128,9216]{1,0:T(8,128)(2,1)S(1)} %copy-done, bf16[32,144,128]{2,1,0:T(8,128)(2,1)S(1)} %gather_keys.1.kv, f32[512,128]{1,0:T(8,128)S(1)} %copy-done.4, bf16[16,512,128]{2,1,0:T(8,128)(2,1)S(1)} %copy-done.1), custom_call_target="tpu_custom_call" | custom-call | flops 4294967296 | bytes 8388608 | tf_op jit(solution)/shard_map/attend/pallas_call | solution.py:400
Async XLA Ops:
  0.0 15.3 %copy-start.1 = (bf16[16,512,128]{2,1,0:T(8,128)(2,1)S(1)}, bf16[16,512,128]{2,1,0:T(8,128)(2,1)}, u32[]{:S(2)}) copy-start(bf16[16,512,128]{2,1,0:T(8,128)(2,1)} %w_ref.1) | copy-start | bytes 6291460
  0.0 15.3 %copy-start = (bf16[128,9216]{1,0:T(8,128)(2,1)S(1)}, bf16[128,9216]{1,0:T(8,128)(2,1)}, u32[]{:S(2)}) copy-start(bf16[128,9216]{1,0:T(8,128)(2,1)} %queries_ref.1) | copy-start | bytes 7077892
  0.0 0.9 %copy-start.2 = (bf16[32,576]{1,0:T(8,128)(2,1)S(1)}, bf16[32,576]{1,0:T(8,128)(2,1)}, u32[]{:S(2)}) copy-start(bf16[32,576]{1,0:T(8,128)(2,1)} %latent_ref.1) | copy-start | bytes 110596
  0.9 14.4 %copy-start.3 = (s32[16]{0:T(128)S(1)}, s32[16]{0:T(128)}, u32[]{:S(2)}) copy-start(s32[16]{0:T(128)} %order_hbm.1) | copy-start | bytes 196
  0.9 14.4 %copy-start.4 = (f32[512,128]{1,0:T(8,128)S(1)}, f32[512,128]{1,0:T(8,128)}, u32[]{:S(2)}) copy-start(f32[512,128]{1,0:T(8,128)} %constant.2.clone.table) | copy-start | bytes 786436

commit v5 on v4

--- a/solution.py
+++ b/solution.py
@@ -87,7 +87,9 @@
     mesh_id = pl.DeviceIdType.MESH
     barrier = pltpu.get_barrier_semaphore()
     peers = [(d, 0) for d in far] + [(0, k) for k in range(1, n_head)] + [(1, 0)]
-    peers.sort(key=lambda peer: bin(peer[0]).count("1") + (peer[1] + peer[1] // 2) * 0.9)
+    peers.sort(
+        key=lambda peer: bin(peer[0]).count("1") + (peer[1] + peer[1] // 2) * 1.05 + 0.1 * (peer[0] == 1)
+    )
 
     def signal(sem, d, k):
         pl.semaphore_signal(

time: 20.7 us -> 20.7 us (level)
  no operation moved by 1% of the time
where the time goes in v5:
time: 20.7 us; the launch traced here: 20.6 us
  Pallas kernels  19.6 us (95%)
  local copies, waits for them, and re-layouts  0.94 us (5%)
    pallas_call x1, Pallas kernels, per_device(): pl.pallas_call(functools.partial(gather_kernel, dims), out_shape=jax.Shap...  14.4 us
    pallas_call x1, Pallas kernels, per_device(): pl.pallas_call(functools.partial(attend_kernel, dims), out_shape=jax.Shap...  5.2 us
    unnamed x10, local copies, waits for them, and re-layouts  0.94 us

profile of v5, /device:TPU:0, one launch (start us, length us, event | category | flops | bytes accessed | tf_op | source)
XLA Modules:
  0.0 20.6 jit_solution(17999752627772671502)
XLA Ops:
  0.0 0.0 copy-start.1
  0.0 0.0 copy-start
  0.0 0.0 copy-start.2
  0.0 0.9 %copy-done.2 = bf16[32,576]{1,0:T(8,128)(2,1)S(1)} copy-done((bf16[32,576]{1,0:T(8,128)(2,1)S(1)}, bf16[32,576]{1,0:T(8,128)(2,1)}, u32[]{:S(2)}) %copy-start.2) | copy-done | bytes 36888
  0.9 0.0 copy-start.3
  0.9 0.0 copy-start.4
  0.9 14.4 %gather_keys.1.kv = bf16[32,144,128]{2,1,0:T(8,128)(2,1)S(1)} custom-call(bf16[32,576]{1,0:T(8,128)(2,1)S(1)} %copy-done.2), custom_call_target="tpu_custom_call" | custom-call | flops 21474836480 | bytes 1048576 | tf_op jit(solution)/shard_map/gather_keys/pallas_call | solution.py:382
  15.3 0.0 copy-done.1
  15.3 0.0 copy-done
  15.3 0.0 copy-done.3
  15.4 0.0 copy-done.4
  15.4 5.2 %attend.1 = bf16[128,2048]{1,0:T(8,128)(2,1)} custom-call(s32[16]{0:T(128)S(1)} %copy-done.3, bf16[128,9216]{1,0:T(8,128)(2,1)S(1)} %copy-done, bf16[32,144,128]{2,1,0:T(8,128)(2,1)S(1)} %gather_keys.1.kv, f32[512,128]{1,0:T(8,128)S(1)} %copy-done.4, bf16[16,512,128]{2,1,0:T(8,128)(2,1)S(1)} %copy-done.1), custom_call_target="tpu_custom_call" | custom-call | flops 4294967296 | bytes 8388608 | tf_op jit(solution)/shard_map/attend/pallas_call | solution.py:402
Async XLA Ops:
  0.0 15.3 %copy-start.1 = (bf16[16,512,128]{2,1,0:T(8,128)(2,1)S(1)}, bf16[16,512,128]{2,1,0:T(8,128)(2,1)}, u32[]{:S(2)}) copy-start(bf16[16,512,128]{2,1,0:T(8,128)(2,1)} %w_ref.1) | copy-start | bytes 6291460
  0.0 15.3 %copy-start = (bf16[128,9216]{1,0:T(8,128)(2,1)S(1)}, bf16[128,9216]{1,0:T(8,128)(2,1)}, u32[]{:S(2)}) copy-start(bf16[128,9216]{1,0:T(8,128)(2,1)} %queries_ref.1) | copy-start | bytes 7077892
  0.0 0.9 %copy-start.2 = (bf16[32,576]{1,0:T(8,128)(2,1)S(1)}, bf16[32,576]{1,0:T(8,128)(2,1)}, u32[]{:S(2)}) copy-start(bf16[32,576]{1,0:T(8,128)(2,1)} %latent_ref.1) | copy-start | bytes 110596
  0.9 14.4 %copy-start.3 = (s32[16]{0:T(128)S(1)}, s32[16]{0:T(128)}, u32[]{:S(2)}) copy-start(s32[16]{0:T(128)} %order_hbm.1) | copy-start | bytes 196
  0.9 14.4 %copy-start.4 = (f32[512,128]{1,0:T(8,128)S(1)}, f32[512,128]{1,0:T(8,128)}, u32[]{:S(2)}) copy-start(f32[512,128]{1,0:T(8,128)} %constant.2.clone.table) | copy-start | bytes 786436
